TPU v7x, 32 devices: a whole 2x2x4 slice. The times are simulated.
32 devices in a mesh: part: 2 (over x), loc: 4 (over z), grp: 4 (over y, core).
Axes of the slice: x: 2, y: 2, z: 4, core: 2. Of those that a mesh axis runs over, the one named last changes fastest.
Arguments:
- x_rows: bfloat16 [49152, 512], P(('part', 'grp', 'loc')), parts along dimension 0
- dy_rows: bfloat16 [49152, 512], P(('part', 'grp', 'loc')), parts along dimension 0
- expert_ids: int32 [49152, 4], P(('part', 'grp', 'loc')), parts along dimension 0
- gate_vals: float32 [49152, 4], P(('part', 'grp', 'loc')), parts along dimension 0
- w_gate: bfloat16 [32, 512, 896], P(('part', 'grp', 'loc')), parts along dimension 0
- w_up: bfloat16 [32, 512, 896], P(('part', 'grp', 'loc')), parts along dimension 0
- w_down: bfloat16 [32, 896, 512], P(('part', 'grp', 'loc')), parts along dimension 0
Outputs:
- output 1: bfloat16 [49152, 512], P(('part', 'grp', 'loc')), parts along dimension 0
- output 2: float32 [49152, 4], P(('part', 'grp', 'loc')), parts along dimension 0
- output 3: bfloat16 [32, 512, 896], P(('part', 'grp', 'loc')), parts along dimension 0
- output 4: bfloat16 [32, 512, 896], P(('part', 'grp', 'loc')), parts along dimension 0
- output 5: bfloat16 [32, 896, 512], P(('part', 'grp', 'loc')), parts along dimension 0
There are 2 independent parts. A program takes and returns all parts, laid end to end along the dimension named above; each array names one.
All inputs are finite; a program needn't handle non-finite values.
Results may differ from a plain program's by a relative error of at most 0.001.
Values are sent between devices in bfloat16 or wider.
A program may use at most 1 GiB of HBM per device.

v0:
```python
import jax
import jax.numpy as jnp
from jax import lax
from jax.sharding import PartitionSpec as P


def slot_table(bin_ids, num_bins, capacity):
    n_items = bin_ids.shape[0]
    item_order = jnp.argsort(bin_ids, stable=True)
    sorted_bins = bin_ids[item_order]
    bin_sizes = jax.ops.segment_sum(jnp.ones_like(bin_ids), bin_ids, num_segments=num_bins + 1)
    bin_starts = jnp.cumsum(bin_sizes) - bin_sizes
    slot_rank = jnp.arange(n_items, dtype=jnp.int32) - bin_starts[sorted_bins]
    dest_slot = jnp.where(sorted_bins < num_bins, sorted_bins * capacity + slot_rank, num_bins * capacity)
    slot_grid = jnp.full((num_bins * capacity + 1,), n_items, jnp.int32).at[dest_slot].set(item_order.astype(jnp.int32))
    return slot_grid[:num_bins * capacity].reshape(num_bins, capacity)


def gather_rows(source, row_index, fill_val):
    return jnp.take(source, row_index, axis=0, mode='fill', fill_value=fill_val)


def first_in_group(dest_group):
    top_k = dest_group.shape[-1]
    same_group = dest_group[..., :, None] == dest_group[..., None, :]
    earlier = jnp.arange(top_k)[None, :] < jnp.arange(top_k)[:, None]
    return same_group, jnp.logical_not(jnp.any(same_group & earlier, axis=-1))


def expert_backward(x_own, dy_own, gate_own, w_gate, w_up, w_down, row_axes, wt_axes):
    up_form = row_axes + 'd,' + wt_axes + 'df->' + row_axes + 'f'
    down_form = row_axes + 'f,' + wt_axes + 'fd->' + row_axes + 'd'
    back_form = row_axes + 'd,' + wt_axes + 'fd->' + row_axes + 'f'
    tr_form = row_axes + 'f,' + wt_axes + 'df->' + row_axes + 'd'
    grad_down = row_axes + 'f,' + row_axes + 'd->' + wt_axes + 'fd'
    grad_up = row_axes + 'd,' + row_axes + 'f->' + wt_axes + 'df'
    pre_gate = jnp.einsum(up_form, x_own, w_gate, preferred_element_type=jnp.float32)
    pre_up = jnp.einsum(up_form, x_own, w_up, preferred_element_type=jnp.float32)
    sig_gate = jax.nn.sigmoid(pre_gate)
    silu_out = pre_gate * sig_gate
    hidden = (silu_out * pre_up).astype(jnp.bfloat16)
    expert_out = jnp.einsum(down_form, hidden, w_down, preferred_element_type=jnp.float32)
    d_gate = jnp.sum(dy_own * expert_out, axis=-1)
    d_out = (gate_own[..., None] * dy_own).astype(jnp.bfloat16)
    d_hidden = jnp.einsum(back_form, d_out, w_down, preferred_element_type=jnp.float32)
    dw_down = jnp.einsum(grad_down, hidden, d_out, preferred_element_type=jnp.float32).astype(jnp.bfloat16)
    d_pre_up = (d_hidden * silu_out).astype(jnp.bfloat16)
    d_pre_gate = (d_hidden * pre_up * sig_gate * (1.0 + pre_gate * (1.0 - sig_gate))).astype(jnp.bfloat16)
    dw_gate = jnp.einsum(grad_up, x_own, d_pre_gate, preferred_element_type=jnp.float32).astype(jnp.bfloat16)
    dw_up = jnp.einsum(grad_up, x_own, d_pre_up, preferred_element_type=jnp.float32).astype(jnp.bfloat16)
    d_x = (jnp.einsum(tr_form, d_pre_gate, w_gate, preferred_element_type=jnp.float32) + jnp.einsum(tr_form, d_pre_up, w_up, preferred_element_type=jnp.float32)).astype(jnp.bfloat16)
    return d_x, d_gate, dw_gate, dw_up, dw_down


def solution(mesh):
    grp_size = mesh.shape['grp']
    loc_size = mesh.shape['loc']
    spec = P(('part', 'grp', 'loc'))

    def device_step(x_rows, dy_rows, expert_ids, gate_vals, w_gate, w_up, w_down):
        n_tok, d_model = x_rows.shape
        top_k = expert_ids.shape[1]
        local_experts = w_gate.shape[0]
        group_experts = local_experts * loc_size
        num_experts = group_experts * grp_size
        group_limit = min(top_k // 2, grp_size)
        group_rows = group_limit * n_tok // grp_size
        src_cap = min(2 * (n_tok * top_k // num_experts), group_rows)
        relay_cap = grp_size * src_cap
        rows_in = grp_size * group_rows
        my_group = lax.axis_index('grp')

        dest_group = expert_ids // group_experts
        same_group, first_slot = first_in_group(dest_group)
        send_items = slot_table(jnp.where(first_slot, dest_group, grp_size).reshape(-1), grp_size, group_rows)
        send_tok = send_items // top_k
        x_recv = lax.all_to_all(gather_rows(x_rows, send_tok, 0), 'grp', 0, 0).reshape(rows_in, d_model)
        dy_recv = lax.all_to_all(gather_rows(dy_rows, send_tok, 0), 'grp', 0, 0).reshape(rows_in, d_model)
        ids_recv = lax.all_to_all(gather_rows(expert_ids, send_tok, -1), 'grp', 0, 0).reshape(rows_in, top_k)
        gate_recv = lax.all_to_all(gather_rows(gate_vals, send_tok, 0), 'grp', 0, 0).reshape(rows_in * top_k)

        local_ids = ids_recv - my_group * group_experts
        is_mine = (local_ids >= 0) & (local_ids < group_experts)
        fan_items = slot_table(jnp.where(is_mine, local_ids, group_experts).reshape(-1), group_experts, relay_cap)
        fan_rows = fan_items // top_k
        own_shape = (loc_size, local_experts, relay_cap)
        x_own = lax.all_to_all(gather_rows(x_recv, fan_rows, 0).reshape(own_shape + (d_model,)), 'loc', 0, 0)
        dy_own = lax.all_to_all(gather_rows(dy_recv, fan_rows, 0).reshape(own_shape + (d_model,)), 'loc', 0, 0)
        gate_own = lax.all_to_all(gather_rows(gate_recv, fan_items, 0).reshape(own_shape), 'loc', 0, 0)

        d_x, d_gate, dw_gate, dw_up, dw_down = expert_backward(x_own, dy_own, gate_own, w_gate, w_up, w_down, 'lec', 'e')

        contrib_back = lax.all_to_all(d_x, 'loc', 0, 0).reshape(group_experts * relay_cap, d_model)
        dgate_back = lax.all_to_all(d_gate, 'loc', 0, 0).reshape(-1)
        group_sum = jax.ops.segment_sum(contrib_back.astype(jnp.float32), fan_rows.reshape(-1), num_segments=rows_in + 1)
        group_part = group_sum[:rows_in].astype(jnp.bfloat16).reshape(grp_size, group_rows, d_model)
        dgate_rel = jax.ops.segment_sum(dgate_back, fan_items.reshape(-1), num_segments=rows_in * top_k + 1)
        dgate_rel = dgate_rel[:rows_in * top_k].reshape(grp_size, group_rows, top_k)
        part_home = lax.all_to_all(group_part, 'grp', 0, 0).reshape(rows_in, d_model)
        dgate_home = lax.all_to_all(dgate_rel, 'grp', 0, 0).reshape(rows_in, top_k)

        home_tok = send_tok.reshape(-1)
        dx_sum = jax.ops.segment_sum(part_home.astype(jnp.float32), home_tok, num_segments=n_tok + 1)
        d_gates = jax.ops.segment_sum(dgate_home, home_tok, num_segments=n_tok + 1)[:n_tok]
        return dx_sum[:n_tok].astype(jnp.bfloat16), d_gates, dw_gate, dw_up, dw_down

    return jax.shard_map(device_step, mesh=mesh, in_specs=(spec,) * 7, out_specs=(spec,) * 5, check_vma=False)
```

profile of v0, /device:TPU:0, one launch (start us, length us, event | category | flops | bytes accessed | tf_op | source)
XLA Modules:
  0.0 1809.3 jit_solution(11602889797288182417)
XLA Ops:
  3.2 42.9 %scatter_custom_fusion = s32[5]{0:T(128)S(1)} fusion(s32[6144]{0:T(1024)S(1)} %reshape.511, s32[6144]{0:T(1024)S(1)} %broadcast.400, s32[]{:T(128)} %constant.78.clone.1), kind=kCustom, calls=%fused_computation.176 | custom fusion | flops 6144 | bytes 24 | tf_op jit(solution)/shard_map/scatter-add | solution.py:11
  47.0 6.7 sort.34
  53.7 34.3 %gather_fusion = s32[6144]{0:T(1024)S(1)} fusion(s32[6144]{0:T(1024)S(1)} %reshape.511, s32[6144]{0:T(1024)S(1)} %fusion.78), kind=kCustom, calls=%fused_computation.4 | custom fusion | bytes 73728 | tf_op jit(solution)/shard_map/gather | solution.py:10
  88.0 3.4 compare_select_fusion.8
  91.4 23.0 %scatter_custom_fusion.1 = s32[3073]{0:T(1024)S(1)} fusion(s32[6144]{0:T(1024)S(1)} %bitcast.240, s32[6144]{0:T(1024)S(1)} %get-tuple-element.9, s32[]{:T(128)} %constant.70.clone.1), kind=kCustom, calls=%fused_computation.167 | custom fusion | bytes 12296 | tf_op jit(solution)/shard_map/scatter | solution.py:15
  115.5 10.9 gather_fusion.1
  128.9 4.3 all-to-all-start
  133.6 10.9 gather_fusion.3
  146.4 13.2 gather_fusion.7
  159.6 13.2 gather_fusion.5
  172.8 4.9 broadcast_select_fusion.1
  178.3 14.9 all-to-all-start.1
  196.1 85.2 %scatter_custom_fusion.2 = s32[5]{0:T(128)S(1)} fusion(s32[12288]{0:T(1024)S(1)} %bitcast.239, s32[12288]{0:T(1024)S(1)} %broadcast.401, s32[]{:T(128)} %constant.78.clone.1), kind=kCustom, calls=%fused_computation.174 | custom fusion | flops 12288 | bytes 24 | tf_op jit(solution)/shard_map/scatter-add | solution.py:11
  281.5 8.2 sort.35
  290.3 68.0 %gather_fusion.2 = s32[12288]{0:T(1024)S(1)} fusion(s32[12288]{0:T(1024)S(1)} %and_select_fusion.2, s32[12288]{0:T(1024)S(1)} %fusion.67), kind=kCustom, calls=%fused_computation.6 | custom fusion | bytes 147456 | tf_op jit(solution)/shard_map/gather | solution.py:10
  358.4 3.7 all-to-all-start.5
  362.1 3.4 compare_select_fusion.1
  365.5 45.4 %scatter_custom_fusion.3 = s32[12289]{0:T(1024)S(1)} fusion(s32[12288]{0:T(1024)S(1)} %bitcast.238, s32[12288]{0:T(1024)S(1)} %get-tuple-element.10, s32[]{:T(128)} %constant.96.clone.1), kind=kCustom, calls=%fused_computation.131 | custom fusion | bytes 49160 | tf_op jit(solution)/shard_map/scatter | solution.py:15
  411.6 4.7 all-to-all-start.3
  420.7 68.0 %gather_fusion.4 = f32[12288]{0:T(1024)S(1)} fusion(f32[12288]{0:T(1024)S(1)} %reshape.519, s32[12288]{0:T(1024)S(1)} %broadcast_clamp_fusion.1), kind=kCustom, calls=%fused_computation.8 | custom fusion | bytes 147456 | tf_op jit(solution)/shard_map/jit(_take)/gather | solution.py:20
  489.5 49.8 %gather_fusion.8 = bf16[12288,512]{1,0:T(8,128)(2,1)} fusion(bf16[3072,512]{1,0:T(8,128)(2,1)S(1)} %bitcast.218, s32[12288]{0:T(1024)S(1)} %broadcast_clamp_fusion), kind=kCustom, calls=%fused_computation.3.clone | custom fusion | bytes 25214976 | tf_op jit(solution)/shard_map/jit(_take)/gather | solution.py:20
  539.3 5.4 all-to-all-start.2
  544.7 52.5 %gather_fusion.6 = bf16[12288,512]{1,0:T(8,128)(2,1)} fusion(bf16[3072,512]{1,0:T(8,128)(2,1)} %bitcast.24, s32[12288]{0:T(1024)S(1)} %broadcast_clamp_fusion), kind=kCustom, calls=%fused_computation.1.clone | custom fusion | bytes 25214976 | tf_op jit(solution)/shard_map/jit(_take)/gather | solution.py:20
  597.1 17.4 select_bitcast_fusion.1
  614.6 6.4 all-to-all-start.6
  620.9 16.6 copy.86
  637.6 256.5 %all-to-all-done.6 = bf16[4,1,3072,512]{3,2,1,0:T(8,128)(2,1)} async-done(((bf16[4,1,3072,512]{3,2,1,0:T(8,128)(2,1)}), bf16[4,1,3072,512]{3,2,1,0:T(8,128)(2,1)}, u32[]{:S(2)}, u32[]{:S(2)}) %all-to-all-start.6) | async-done | bytes 12582944 | tf_op jit(solution)/shard_map/all_to_all | solution.py:87
  894.1 6.7 all-to-all-start.4
  900.9 22.9 %fusion.24 = f32[4,3072,896]{2,1,0:T(8,128)} fusion(bf16[4,1,3072,512]{3,2,1,0:T(8,128)(2,1)} %all-to-all-done.6, bf16[1,512,896]{2,1,0:T(8,128)(2,1)S(1)} %copy-done.9), kind=kOutput, calls=%fused_computation.50 | convolution fusion | flops 11274289152 | bytes 57540608 | tf_op jit(solution)/shard_map/lecd,edf->lecf/dot_general | solution.py:37
  923.8 249.4 %all-to-all-done.4 = bf16[4,1,3072,512]{2,3,1,0:T(8,128)(2,1)} async-done(((bf16[4,1,3072,512]{2,3,1,0:T(8,128)(2,1)}), bf16[4,1,3072,512]{2,3,1,0:T(8,128)(2,1)}, u32[]{:S(2)}, u32[]{:S(2)}) %all-to-all-start.4) | async-done | bytes 12582944 | tf_op jit(solution)/shard_map/all_to_all | solution.py:88
  1173.1 24.6 %fusion.30 = f32[4,3072,896]{2,1,0:T(8,128)} fusion(bf16[4,1,3072,512]{2,3,1,0:T(8,128)(2,1)} %all-to-all-done.4, f32[4,3072]{1,0:T(4,128)S(1)} %bitcast.235, bf16[1,896,512]{2,1,0:T(8,128)(2,1)S(1)} %copy-done.8), kind=kOutput, calls=%fused_computation.57 | convolution fusion | flops 11293163520 | bytes 57589760 | tf_op jit(solution)/shard_map/lecd,efd->lecf/dot_general | solution.py:45
  1197.7 61.7 %fusion.14 = (bf16[4,3072,896]{2,1,0:T(8,128)(2,1)}, bf16[4,1,3072,896]{3,2,0,1:T(8,128)(2,1)}, bf16[4,3072,896]{2,1,0:T(8,128)(2,1)}) fusion(f32[4,3072,896]{2,1,0:T(8,128)} %fusion.24, f32[4,3072,896]{2,1,0:T(8,128)} %fusion.30, bf16[1,512,896]{2,1,0:T(8,128)(2,1)S(1)} %copy-done.10, bf16[4,1,3072,512]{3,2,1,0:T(8,128)(2,1)} %all-to-all-done.6), kind=kOutput, calls=%fused_computation.40 | convolution fusion | flops 11439439872 | bytes 167641088 | tf_op jit(solution)/shard_map/lecd,edf->lecf/dot_general | solution.py:38
  1259.4 18.5 %fusion.10 = f32[4,3072]{1,0:T(4,128)S(1)} fusion(bf16[4,1,3072,512]{2,3,1,0:T(8,128)(2,1)} %all-to-all-done.4, bf16[4,3072,896]{2,1,0:T(8,128)(2,1)} %get-tuple-element.35, bf16[1,896,512]{2,1,0:T(8,128)(2,1)S(1)} %copy-done.8), kind=kOutput, calls=%fused_computation.35 | convolution fusion | flops 11293151232 | bytes 35569664 | tf_op jit(solution)/shard_map/lecf,efd->lecd/dot_general | solution.py:42
  1278.6 3.3 all-to-all-start.9
  1281.9 22.2 %fusion.17 = f32[4,3072,512]{2,1,0:T(8,128)} fusion(bf16[4,1,3072,896]{3,2,0,1:T(8,128)(2,1)} %get-tuple-element.36, bf16[1,512,896]{2,1,0:T(8,128)(2,1)S(1)} %copy-done.9), kind=kOutput, calls=%fused_computation.43 | convolution fusion | flops 11274289152 | bytes 48103424 | tf_op jit(solution)/shard_map/lecf,edf->lecd/dot_general | solution.py:51
  1304.1 25.2 %fusion.19 = bf16[4,1,3072,512]{3,2,1,0:T(8,128)(2,1)} fusion(f32[4,3072,512]{2,1,0:T(8,128)} %fusion.17, bf16[4,3072,896]{2,1,0:T(8,128)(2,1)} %get-tuple-element.37, bf16[1,512,896]{2,1,0:T(8,128)(2,1)S(1)} %copy-done.10), kind=kOutput, calls=%fused_computation.45 | convolution fusion | flops 11286872064 | bytes 60686336 | tf_op jit(solution)/shard_map/lecf,edf->lecd/dot_general | solution.py:51
  1329.3 6.7 all-to-all-start.7
  1336.0 85.4 %scatter_custom_fusion.6 = f32[12289]{0:T(1024)S(1)} fusion(s32[12288]{0:T(1024)} %copy-done.3, f32[12288]{0:T(1024)S(1)} %bitcast.237, f32[]{:T(128)} %constant.69.clone.1), kind=kCustom, calls=%fused_computation.129 | custom fusion | flops 12288 | bytes 49668 | tf_op jit(solution)/shard_map/scatter-add | solution.py:97
  1424.1 184.1 %all-to-all-done.7 = bf16[4,1,3072,512]{3,2,1,0:T(8,128)(2,1)} async-done(((bf16[4,1,3072,512]{3,2,1,0:T(8,128)(2,1)}), bf16[4,1,3072,512]{3,2,1,0:T(8,128)(2,1)}, u32[]{:S(2)}, u32[]{:S(2)}) %all-to-all-start.7) | async-done | bytes 12582944 | tf_op jit(solution)/shard_map/all_to_all | solution.py:93
  1608.2 3.3 all-to-all-start.10
  1611.5 20.3 %fusion.44 = bf16[1,512,896]{2,1,0:T(8,128)(2,1)} fusion(bf16[4,1,3072,896]{3,2,0,1:T(8,128)(2,1)} %get-tuple-element.36, bf16[4,1,3072,512]{3,2,1,0:T(8,128)(2,1)} %all-to-all-done.6), kind=kOutput, calls=%fused_computation.69 | convolution fusion | flops 11274747904 | bytes 35520512 | tf_op jit(solution)/shard_map/lecd,lecf->edf/dot_general | solution.py:49
  1631.8 83.7 %scatter_custom_fusion.4 = f32[3073,512]{1,0:T(8,128)} fusion(s32[12288]{0:T(1024)} %get-tuple-element.39, bf16[12288,512]{1,0:T(8,128)(2,1)} %bitcast.80, f32[]{:T(128)} %constant.69.clone.1), kind=kCustom, calls=%fused_computation.36 | custom fusion | flops 12582912 | bytes 18876928 | tf_op jit(solution)/shard_map/scatter-add | solution.py:95
  1715.5 4.9 slice.66
  1720.4 4.8 all-to-all-start.8
  1725.2 20.3 %fusion.49 = bf16[1,512,896]{2,1,0:T(8,128)(2,1)} fusion(bf16[4,3072,896]{2,1,0:T(8,128)(2,1)} %get-tuple-element.37, bf16[4,1,3072,512]{3,2,1,0:T(8,128)(2,1)} %all-to-all-done.6), kind=kOutput, calls=%fused_computation.70 | convolution fusion | flops 11274747904 | bytes 35520512 | tf_op jit(solution)/shard_map/lecd,lecf->edf/dot_general | solution.py:50
  1745.5 18.9 %fusion.52 = bf16[1,896,512]{2,1,0:T(8,128)(2,1)} fusion(bf16[4,3072,896]{2,1,0:T(8,128)(2,1)} %get-tuple-element.35, bf16[4,1,3072,512]{2,3,1,0:T(8,128)(2,1)} %all-to-all-done.4, f32[4,3072]{1,0:T(4,128)S(1)} %bitcast.236), kind=kOutput, calls=%fused_computation.71 | convolution fusion | flops 11293622272 | bytes 35569664 | tf_op jit(solution)/shard_map/lecf,lecd->efd/dot_general | solution.py:46
  1766.1 17.6 scatter_custom_fusion.7
  1784.6 21.3 %scatter_custom_fusion.5 = f32[1537,512]{1,0:T(8,128)} fusion(s32[3072]{0:T(1024)} %get-tuple-element.41, bf16[3072,512]{1,0:T(8,128)(2,1)} %bitcast.81, f32[]{:T(128)} %constant.69.clone.1), kind=kCustom, calls=%fused_computation.59 | custom fusion | flops 3145728 | bytes 6294016 | tf_op jit(solution)/shard_map/scatter-add | solution.py:103
  (90 shorter events, 28.4 us)
Async XLA Ops:
  0.6 145.7 %copy-start = (bf16[1536,512]{1,0:T(8,128)(2,1)S(1)}, bf16[1536,512]{1,0:T(8,128)(2,1)}, u32[]{:S(2)}) copy-start(bf16[1536,512]{1,0:T(8,128)(2,1)} %param.11) | copy-start | bytes 4718596
  53.7 61.4 %copy-start.4 = (s32[1536,4]{0,1:T(4,128)S(1)}, s32[1536,4]{0,1:T(4,128)}, u32[]{:S(2)}) copy-start(s32[1536,4]{0,1:T(4,128)} %param.13) | copy-start | bytes 73732
  88.0 45.2 %copy-start.7 = (f32[1536,4]{0,1:T(4,128)S(1)}, f32[1536,4]{0,1:T(4,128)}, u32[]{:S(2)}) copy-start(f32[1536,4]{0,1:T(4,128)} %param.14) | copy-start | bytes 73732
  128.9 49.4 %all-to-all-start = ((s32[4,768,4]{1,2,0:T(4,128)}), s32[4,768,4]{1,2,0:T(4,128)S(1)}, u32[]{:S(2)}, u32[]{:S(2)}) async-start(s32[4,768,4]{1,2,0:T(4,128)} %broadcast_select_fusion.3), calls=%async_computation | async-start | bytes 98304 | tf_op jit(solution)/shard_map/all_to_all | solution.py:79
  146.4 13.2 copy-start.2
  178.3 180.0 %all-to-all-start.1 = ((f32[4,768,4]{1,2,0:T(4,128)}), f32[4,768,4]{1,2,0:T(4,128)S(1)}, u32[]{:S(2)}, u32[]{:S(2)}) async-start(f32[4,768,4]{1,2,0:T(4,128)} %broadcast_select_fusion.2), calls=%async_computation.1 | async-start | bytes 98304 | tf_op jit(solution)/shard_map/all_to_all | solution.py:80
  358.4 53.2 %all-to-all-start.5 = ((bf16[4,768,512]{2,1,0:T(8,128)(2,1)}), bf16[4,768,512]{2,1,0:T(8,128)(2,1)S(1)}, u32[]{:S(2)}, u32[]{:S(2)}) async-start(bf16[4,768,512]{2,1,0:T(8,128)(2,1)} %get-tuple-element.45), calls=%async_computation.5 | async-start | bytes 6291456 | tf_op jit(solution)/shard_map/all_to_all | solution.py:77
  411.6 77.1 %copy-start.3 = (s32[12288]{0:T(1024)}, s32[12288]{0:T(1024)S(1)}, u32[]{:S(2)}) copy-start(s32[12288]{0:T(1024)S(1)} %get-tuple-element.38) | copy-start | bytes 147460
  411.6 127.7 %all-to-all-start.3 = ((bf16[4,768,512]{2,1,0:T(8,128)(2,1)}), bf16[4,768,512]{2,1,0:T(8,128)(2,1)}, u32[]{:S(2)}, u32[]{:S(2)}) async-start(bf16[4,768,512]{2,1,0:T(8,128)(2,1)} %get-tuple-element.44), calls=%async_computation.3 | async-start | bytes 6291456 | tf_op jit(solution)/shard_map/all_to_all | solution.py:78
  539.3 75.3 %all-to-all-start.2 = ((f32[4,1,3072]{2,1,0:T(1,128)}), f32[4,1,3072]{2,1,0:T(1,128)S(1)}, u32[]{:S(2)}, u32[]{:S(2)}) async-start(f32[4,1,3072]{2,1,0:T(1,128)} %and_select_fusion), calls=%async_computation.2 | async-start | bytes 98304 | tf_op jit(solution)/shard_map/all_to_all | solution.py:89
  614.6 279.5 %all-to-all-start.6 = ((bf16[4,1,3072,512]{3,2,1,0:T(8,128)(2,1)}), bf16[4,1,3072,512]{3,2,1,0:T(8,128)(2,1)}, u32[]{:S(2)}, u32[]{:S(2)}) async-start(bf16[4,1,3072,512]{3,2,1,0:T(8,128)(2,1)} %get-tuple-element.43), calls=%async_computation.6 | async-start | bytes 25165824 | tf_op jit(solution)/shard_map/all_to_all | solution.py:87
  637.6 263.3 %copy-start.9 = (bf16[1,512,896]{2,1,0:T(8,128)(2,1)S(1)}, bf16[1,512,896]{2,1,0:T(8,128)(2,1)}, u32[]{:S(2)}) copy-start(bf16[1,512,896]{2,1,0:T(8,128)(2,1)} %param.15) | copy-start | bytes 2752516
  894.1 279.0 %all-to-all-start.4 = ((bf16[4,1,3072,512]{2,3,1,0:T(8,128)(2,1)}), bf16[4,1,3072,512]{2,3,1,0:T(8,128)(2,1)}, u32[]{:S(2)}, u32[]{:S(2)}) async-start(bf16[4,1,3072,512]{2,3,1,0:T(8,128)(2,1)} %copy.86), calls=%async_computation.4 | async-start | bytes 25165824 | tf_op jit(solution)/shard_map/all_to_all | solution.py:88
  900.9 272.3 %copy-start.5 = (f32[4,1,3072]{2,0,1:T(4,128)}, f32[4,1,3072]{2,0,1:T(4,128)S(1)}, u32[]{:S(2)}) copy-start(f32[4,1,3072]{2,0,1:T(4,128)S(1)} %copy.109) | copy-start | bytes 147460
  900.9 272.3 %copy-start.8 = (bf16[1,896,512]{2,1,0:T(8,128)(2,1)S(1)}, bf16[1,896,512]{2,1,0:T(8,128)(2,1)}, u32[]{:S(2)}) copy-start(bf16[1,896,512]{2,1,0:T(8,128)(2,1)} %param.17) | copy-start | bytes 2752516
  1173.1 24.6 %copy-start.10 = (bf16[1,512,896]{2,1,0:T(8,128)(2,1)S(1)}, bf16[1,512,896]{2,1,0:T(8,128)(2,1)}, u32[]{:S(2)}) copy-start(bf16[1,512,896]{2,1,0:T(8,128)(2,1)} %param.16) | copy-start | bytes 2752516
  1278.6 50.7 %all-to-all-start.9 = ((f32[4,1,3072]{2,1,0:T(1,128)}), f32[4,1,3072]{2,1,0:T(1,128)S(1)}, u32[]{:S(2)}, u32[]{:S(2)}) async-start(f32[4,1,3072]{2,1,0:T(1,128)} %reduce_sum.12), calls=%async_computation.9 | async-start | bytes 98304 | tf_op jit(solution)/shard_map/all_to_all | solution.py:94
  1329.3 278.9 %all-to-all-start.7 = ((bf16[4,1,3072,512]{3,2,1,0:T(8,128)(2,1)}), bf16[4,1,3072,512]{3,2,1,0:T(8,128)(2,1)}, u32[]{:S(2)}, u32[]{:S(2)}) async-start(bf16[4,1,3072,512]{3,2,1,0:T(8,128)(2,1)} %fusion.19), calls=%async_computation.7 | async-start | bytes 25165824 | tf_op jit(solution)/shard_map/all_to_all | solution.py:93
  1608.2 112.2 %all-to-all-start.10 = ((f32[4,768,4]{1,2,0:T(4,128)}), f32[4,768,4]{1,2,0:T(4,128)S(1)}, u32[]{:S(2)}, u32[]{:S(2)}) async-start(f32[4,768,4]{1,2,0:T(4,128)} %copy.91), calls=%async_computation.10 | async-start | bytes 98304 | tf_op jit(solution)/shard_map/all_to_all | solution.py:100
  1720.4 64.3 %all-to-all-start.8 = ((bf16[4,768,512]{2,1,0:T(8,128)(2,1)}), bf16[4,768,512]{2,1,0:T(8,128)(2,1)}, u32[]{:S(2)}, u32[]{:S(2)}) async-start(bf16[4,768,512]{2,1,0:T(8,128)(2,1)} %bitcast.60), calls=%async_computation.8 | async-start | bytes 6291456 | tf_op jit(solution)/shard_map/all_to_all | solution.py:99
  1725.2 20.3 %copy-start.6 = (f32[4,1,3072]{2,0,1:T(4,128)S(1)}, f32[4,1,3072]{2,0,1:T(4,128)}, u32[]{:S(2)}) copy-start(f32[4,1,3072]{2,0,1:T(4,128)} %copy-done.5) | copy-start | bytes 147460
  1745.5 63.6 %copy-start.1 = (bf16[1536,512]{1,0:T(8,128)(2,1)S(1)}, bf16[1536,512]{1,0:T(8,128)(2,1)}, u32[]{:S(2)}) copy-start(bf16[1536,512]{1,0:T(8,128)(2,1)} %param.11) | copy-start | bytes 4718596
where the time goes:
time: 1820 us; the launch traced here: 1810 us
  waiting for transfers between devices  690 us (38%)
  local copies, waits for them, and re-layouts  433 us (24%)
  other arithmetic  386 us (21%)
  matrix products  235 us (13%)
  starting transfers between devices  64.2 us (4%)
    all_to_all x1, waiting for transfers between devices, device_step(): lax.all_to_all(gather_rows(x_recv, fan_rows, 0).reshape(own_shape + (d_mo...  257 us
    all_to_all x1, waiting for transfers between devices, device_step(): lax.all_to_all(gather_rows(dy_recv, fan_rows, 0).reshape(own_shape + (d_m...  249 us
    gather x9, local copies, waits for them, and re-layouts, gather_rows(): return jnp.take(source, row_index, axis=0, mode='fill', fill_value=fill_val)  222 us
    all_to_all x1, waiting for transfers between devices, device_step(): lax.all_to_all(d_x, 'loc', 0, 0).reshape(group_experts * relay_cap, d_model)  184 us
    scatter-add x2, other arithmetic, slot_table(): jax.ops.segment_sum(jnp.ones_like(bin_ids), bin_ids, num_segments=num_bin...  128 us
    gather x2, local copies, waits for them, and re-layouts, slot_table(): sorted_bins = bin_ids[item_order]  102 us
    scatter-add x1, other arithmetic, device_step(): jax.ops.segment_sum(dgate_back, fan_items.reshape(-1), num_segments=rows_...  85.4 us
    scatter-add x1, other arithmetic, device_step(): jax.ops.segment_sum(contrib_back.astype(jnp.float32), fan_rows.reshape(-1...  83.7 us
  transfers between devices with their start and end apart: 11, of which 3 were waited for; matrix products, arithmetic and copies ran while one was open for 44% of the time, Pallas kernels for 0%

commit v1 on v0

v1 whole, which is shorter than its diff:
```python
import functools

import jax
import jax.numpy as jnp
from jax import lax
from jax.experimental import pallas as pl
from jax.experimental.pallas import tpu as pltpu
from jax.sharding import PartitionSpec as P

BF = jnp.bfloat16
F32 = jnp.float32
NT = (((1,), (1,)), ((), ()))
TN = (((0,), (0,)), ((), ()))


def expert_kernel(n_tiles, first, valid_ref, blk_ref, meta_ref, wg_ref, wu_ref, wd_ref, *rest):
    if first:
        c_ref, d_ref, acc_ref, xs_ref, us_ref, h_ref, da_ref, db_ref = rest
    else:
        old_ref, c_ref, d_ref, acc_ref, xs_ref, us_ref, h_ref, da_ref, db_ref = rest
    step = pl.program_id(0)
    half = blk_ref.shape[0] // 2
    d_model = blk_ref.shape[1] // 2
    rows = half // n_tiles

    @pl.when(valid_ref[0] == 1)
    def _():
        for tile in range(n_tiles):
            lo = tile * rows
            at = pl.ds(lo, rows)
            gate = meta_ref[at, 0:1]
            code = meta_ref[at, 1:2]
            in_a = code == 1.0
            in_b = code == 2.0

            def pick(col):
                top = blk_ref[pl.ds(lo, rows), pl.ds(col, d_model)].astype(F32)
                low = blk_ref[pl.ds(half + lo, rows), pl.ds(col, d_model)].astype(F32)
                return jnp.where(in_a, top, jnp.where(in_b, low, 0.0))

            x = pick(0).astype(BF)
            dy = pick(d_model)
            u = (gate * dy).astype(BF)
            xs_ref[at, :] = x
            us_ref[at, :] = u
            a = jnp.dot(x, wg_ref[...], preferred_element_type=F32)
            b = jnp.dot(x, wu_ref[...], preferred_element_type=F32)
            sig = jax.nn.sigmoid(a)
            silu = a * sig
            h = (silu * b).astype(BF)
            h_ref[at, :] = h
            o = jnp.dot(h, wd_ref[...], preferred_element_type=F32)
            d_ref[at, :] = jnp.sum(dy * o, axis=1, keepdims=True)
            dh = lax.dot_general(u, wd_ref[...], NT, preferred_element_type=F32)
            db = (dh * silu).astype(BF)
            da = (dh * b * sig * (1.0 + a * (1.0 - sig))).astype(BF)
            da_ref[at, :] = da
            db_ref[at, :] = db
            c = lax.dot_general(da, wg_ref[...], NT, preferred_element_type=F32)
            c = c + lax.dot_general(db, wu_ref[...], NT, preferred_element_type=F32)
            c_ref[at, :] = c.astype(BF)
        terms = ((xs_ref, da_ref), (xs_ref, db_ref), (us_ref, h_ref))
        for k, (left, right) in enumerate(terms):
            part = lax.dot_general(left[...], right[...], TN, preferred_element_type=F32)
            acc_ref[k] = part if first else old_ref[k] + part

    if not first:
        @pl.when(jnp.logical_and(valid_ref[0] == 0, step == 0))
        def _():
            acc_ref[...] = old_ref[...]


def expert_call(blk, meta, wg, wu, wd, acc, valid):
    n_grp, d_model, d_ff = wg.shape
    half = blk.shape[0] // 2
    first = acc is None
    pick = lambda g, v: (g * v[0], 0, 0)
    pick4 = lambda g, v: (g * v[0], 0, 0, 0)
    acc_spec = pl.BlockSpec((None, 3, d_model, d_ff), pick4)
    in_specs = [
        pl.BlockSpec((2 * half, 2 * d_model), lambda g, v: (0, 0)),
        pl.BlockSpec((None, half, 2), pick),
        pl.BlockSpec((None, d_model, d_ff), pick),
        pl.BlockSpec((None, d_model, d_ff), pick),
        pl.BlockSpec((None, d_ff, d_model), pick),
    ]
    args = [valid, blk, meta, wg, wu, wd]
    aliases = {}
    if not first:
        in_specs.append(acc_spec)
        args.append(acc)
        aliases = {6: 2}
    return pl.pallas_call(
        functools.partial(expert_kernel, 3, first),
        grid_spec=pltpu.PrefetchScalarGridSpec(
            num_scalar_prefetch=1,
            grid=(n_grp,),
            in_specs=in_specs,
            out_specs=[
                pl.BlockSpec((None, half, d_model), pick),
                pl.BlockSpec((None, half, 1), pick),
                acc_spec,
            ],
            scratch_shapes=[
                pltpu.VMEM((half, d_model), BF),
                pltpu.VMEM((half, d_model), BF),
                pltpu.VMEM((half, d_ff), BF),
                pltpu.VMEM((half, d_ff), BF),
                pltpu.VMEM((half, d_ff), BF),
            ],
        ),
        out_shape=[
            jax.ShapeDtypeStruct((n_grp, half, d_model), BF),
            jax.ShapeDtypeStruct((n_grp, half, 1), F32),
            jax.ShapeDtypeStruct((n_grp, 3, d_model, d_ff), F32),
        ],
        input_output_aliases=aliases,
        cost_estimate=pl.CostEstimate(
            flops=18 * n_grp * half * d_model * d_ff, bytes_accessed=70_000_000, transcendentals=0),
        compiler_params=pltpu.CompilerParams(dimension_semantics=('arbitrary',), vmem_limit_bytes=63_000_000),
    )(*args)


def add_bf(*terms):
    total = terms[0].astype(F32)
    for term in terms[1:]:
        total = total + term.astype(F32)
    return total.astype(BF)


def solution(mesh):
    grp_size = mesh.shape['grp']
    loc_size = mesh.shape['loc']
    spec = P(('part', 'grp', 'loc'))

    def device_step(x_rows, dy_rows, expert_ids, gate_vals, w_gate, w_up, w_down):
        n_tok, d_model = x_rows.shape
        half = n_tok // 2
        n_exp = grp_size * loc_size
        loc = lax.axis_index('loc')

        groups = expert_ids // loc_size
        in_group = [jnp.any(groups == g, axis=1) for g in range(grp_size)]
        in_a = in_group[0]
        classes = [in_a & in_group[m] for m in (1, 2, 3)]
        classes += [jnp.logical_not(in_a) & jnp.logical_not(in_group[m]) for m in (1, 2, 3)]
        onehot = jnp.stack(classes, axis=1)
        tok = jnp.arange(n_tok, dtype=jnp.int32)
        earlier = (tok[None, :] < tok[:, None]).astype(BF)
        rank = jnp.dot(earlier, onehot.astype(BF), preferred_element_type=F32)
        sizes = jnp.sum(onehot.astype(F32), axis=0)
        off = jnp.cumsum(sizes) - sizes
        pos = jnp.sum(jnp.where(onehot, rank + off[None, :], 0.0), axis=1).astype(jnp.int32)
        to_pos = (tok[:, None] == pos[None, :]).astype(BF)
        blk = jnp.dot(to_pos, jnp.concatenate([x_rows, dy_rows], axis=1), preferred_element_type=F32).astype(BF)

        exp_iota = jnp.arange(n_exp, dtype=jnp.int32)
        hit = expert_ids[:, :, None] == exp_iota[None, None, :]
        gate_tok = jnp.sum(jnp.where(hit, gate_vals[:, :, None], 0.0), axis=1)
        hit_tok = jnp.any(hit, axis=1).astype(F32)
        tok_meta = jnp.concatenate([gate_tok, hit_tok], axis=1)
        pos_meta = jnp.dot(to_pos.astype(F32), tok_meta, precision=lax.Precision.HIGHEST, preferred_element_type=F32)
        gate_pos = pos_meta[:half, :n_exp] + pos_meta[half:, :n_exp]
        code_pos = pos_meta[:half, n_exp:] + 2.0 * pos_meta[half:, n_exp:]
        meta = jnp.concatenate([gate_pos.T, code_pos.T], axis=0)
        meta_all = lax.all_gather(meta, 'loc', axis=0).reshape(loc_size, 2, grp_size, loc_size, half)
        meta_mine = lax.dynamic_index_in_dim(meta_all, loc, axis=3, keepdims=False)
        meta_mine = jnp.transpose(meta_mine, (0, 2, 3, 1))

        wg = lax.all_gather(w_gate, 'grp', axis=0, tiled=True)
        wu = lax.all_gather(w_up, 'grp', axis=0, tiled=True)
        wd = lax.all_gather(w_down, 'grp', axis=0, tiled=True)

        right_of, left_of = [], []
        hop_r, hop_l = blk, blk
        for k in range(1, loc_size):
            hop_r = lax.ppermute(hop_r, 'loc', [(i, i + 1) for i in range(k - 1, loc_size - 1)])
            hop_l = lax.ppermute(hop_l, 'loc', [(i, i - 1) for i in range(1, loc_size - k + 1)])
            right_of.append(hop_r)
            left_of.append(hop_l)

        def run(block, src, ok, acc):
            meta_src = lax.dynamic_index_in_dim(meta_mine, jnp.clip(src, 0, loc_size - 1), axis=0, keepdims=False)
            return expert_call(block, meta_src, wg, wu, wd, acc, ok.astype(jnp.int32).reshape(1))

        c_own, d_own, acc = run(blk, loc, loc >= 0, None)
        c_right, c_left, d_right, d_left = [], [], [], []
        for k in range(1, loc_size):
            c, d, acc = run(right_of[k - 1], loc - k, loc >= k, acc)
            c_right.append(c)
            d_right.append(d)
            c, d, acc = run(left_of[k - 1], loc + k, loc + k < loc_size, acc)
            c_left.append(c)
            d_left.append(d)

        back_l, back_r = None, None
        for k in range(loc_size - 1, 0, -1):
            send = c_right[k - 1] if back_l is None else add_bf(c_right[k - 1], back_l)
            back_l = lax.ppermute(send, 'loc', [(i, i - 1) for i in range(k, loc_size)])
            send = c_left[k - 1] if back_r is None else add_bf(c_left[k - 1], back_r)
            back_r = lax.ppermute(send, 'loc', [(i, i + 1) for i in range(0, loc_size - k)])

        dw = lax.psum_scatter(acc, 'grp', scatter_dimension=0, tiled=True).astype(BF)
        dw_gate = dw[:, 0]
        dw_up = dw[:, 1]
        dw_down = jnp.swapaxes(dw[:, 2], 1, 2)

        code_own = meta[n_exp:].reshape(grp_size, loc_size, half)
        grp_a = jnp.any(code_own == 1.0, axis=1)
        total = c_own.astype(F32) + back_l.astype(F32) + back_r.astype(F32)
        total = lax.reduce_precision(total, exponent_bits=8, mantissa_bits=7)
        dx_a = jnp.sum(jnp.where(grp_a[:, :, None], total, 0.0), axis=0)
        dx_b = jnp.sum(jnp.where(grp_a[:, :, None], 0.0, total), axis=0)
        dx_pos = jnp.concatenate([dx_a, dx_b], axis=0).astype(BF)
        from_pos = (pos[:, None] == tok[None, :]).astype(BF)
        dx = jnp.dot(from_pos, dx_pos, preferred_element_type=F32).astype(BF)

        d_slots = jnp.stack([d_own] + d_right + d_left)[..., 0]
        d_all = lax.all_gather(d_slots, 'loc', axis=0)
        per_loc = []
        for dev in range(loc_size):
            delta = dev - loc
            slot = jnp.where(delta >= 0, delta, loc_size - 1 - delta)
            per_loc.append(lax.dynamic_index_in_dim(d_all[dev], slot, axis=0, keepdims=False))
        d_exp = jnp.stack(per_loc, axis=1)
        d_exp = d_exp.reshape(n_exp, half)
        code_exp = meta[n_exp:]
        d_a = jnp.where(code_exp == 1.0, d_exp, 0.0)
        d_b = jnp.where(code_exp == 2.0, d_exp, 0.0)
        d_pos = jnp.concatenate([d_a, d_b], axis=1)
        d_tok = lax.dot_general(from_pos.astype(F32), d_pos, NT, precision=lax.Precision.HIGHEST, preferred_element_type=F32)
        d_gates = jnp.sum(jnp.where(hit, d_tok[:, None, :], 0.0), axis=2)
        return dx, d_gates, dw_gate, dw_up, dw_down

    return jax.shard_map(device_step, mesh=mesh, in_specs=(spec,) * 7, out_specs=(spec,) * 5, check_vma=False)
```

time: 1820 us -> 620 us (0.34)
  waiting for transfers between devices: 690 us -> 163 us
  local copies, waits for them, and re-layouts: 433 us -> 15.7 us
  other arithmetic: 386 us -> 22.8 us
  matrix products: 235 us -> 20.1 us
  Pallas kernels: 0 us -> 193 us
  blocking collectives: 0 us -> 143 us
  starting transfers between devices: 64.2 us -> 40.5 us
    all_to_all x11 -> x0, waiting for transfers between devices: 690 us -> none  [the longest x1 257 us: device_step(): lax.all_to_all(gather_rows(x_recv, fan_rows, 0).reshape(own_shape + (d_mo...]
    scatter-add x6 -> x0, other arithmetic: 336 us -> none  [the longest x2 128 us: slot_table(): jax.ops.segment_sum(jnp.ones_like(bin_ids), bin_ids, num_segments=num_bin...]
    gather x13 -> x0, local copies, waits for them, and re-layouts: 326 us -> none  [the longest x9 222 us: gather_rows(): return jnp.take(source, row_index, axis=0, mode='fill', fill_value=fill_val)]
    dot_general x9 -> x5, matrix products: 235 us -> 20.1 us  [the longest x1 6.38 us: device_step(): jnp.dot(to_pos, jnp.concatenate([x_rows, dy_rows], axis=1), preferred_ele...]
    pallas_call x0 -> x7, Pallas kernels: none -> 193 us  [expert_call(): pl.pallas_call(functools.partial(expert_kernel, 3, first), grid_spec=pltp...]
    ppermute x0 -> x12, waiting for transfers between devices: none -> 161 us  [the longest x3 119 us: device_step(): lax.ppermute(send, 'loc', [(i, i + 1) for i in range(0, loc_size - k)])]
    all_gather x0 -> x2, blocking collectives: none -> 143 us  [the longest x1 75.5 us: device_step(): lax.all_gather(meta, 'loc', axis=0)]
    scatter x2 -> x0, local copies, waits for them, and re-layouts: 68.4 us -> none  [slot_table(): jnp.full((num_bins * capacity + 1,), n_items, jnp.int32).at[dest_slot]]
  transfers between devices with their start and end apart: 11 -> 16, of which waited for: 3 -> 3; matrix products, arithmetic and copies ran while one was open for 44% -> 9% of each run, Pallas kernels for 0% -> 25%
where the time goes in v1:
time: 620 us; the launch traced here: 612 us
  Pallas kernels  193 us (31%)
  waiting for transfers between devices  163 us (26%)
  blocking collectives  143 us (23%)
  starting transfers between devices  40.5 us (7%)
  other arithmetic  22.8 us (4%)
  matrix products  20.1 us (3%)
  local copies, waits for them, and re-layouts  15.7 us (3%)
  between operations  14.9 us (2%)
    pallas_call x7, Pallas kernels, expert_call(): pl.pallas_call(functools.partial(expert_kernel, 3, first), grid_spec=pltp...  193 us
    ppermute x3, waiting for transfers between devices, device_step(): lax.ppermute(send, 'loc', [(i, i + 1) for i in range(0, loc_size - k)])  119 us
    all_gather x1, blocking collectives, device_step(): lax.all_gather(meta, 'loc', axis=0)  75.5 us
    all_gather x1, blocking collectives, device_step(): d_all = lax.all_gather(d_slots, 'loc', axis=0)  67.1 us
    ppermute x3, waiting for transfers between devices, device_step(): lax.ppermute(hop_l, 'loc', [(i, i - 1) for i in range(1, loc_size - k + 1)])  42.1 us
    ppermute x3, starting transfers between devices, device_step(): lax.ppermute(send, 'loc', [(i, i + 1) for i in range(0, loc_size - k)])  21.8 us
    unnamed x54, local copies, waits for them, and re-layouts  13.7 us
  transfers between devices with their start and end apart: 16, of which 3 were waited for; matrix products, arithmetic and copies ran while one was open for 9% of the time, Pallas kernels for 25%

profile of v1, /device:TPU:0, one launch (start us, length us, event | category | flops | bytes accessed | tf_op | source)
XLA Modules:
  0.0 612.2 jit_solution(3479867901912894664)
XLA Ops:
  9.4 0.8 compare_reduce_fusion
  10.8 0.9 fusion.19
  11.8 6.4 %fusion.9.blk_ref = bf16[1536,1024]{1,0:T(8,128)(2,1)} fusion(s32[1536]{0:T(1024)S(1)} %convert_element_type.86, bf16[1536,512]{1,0:T(8,128)(2,1)S(1)} %copy-done.18, bf16[1536,512]{1,0:T(8,128)(2,1)S(1)} %copy-done.19), kind=kOutput, calls=%fused_computation.19 | convolution fusion | flops 4842061824 | bytes 6297600 | tf_op jit(solution)/shard_map/dot_general | solution.py:155
  18.2 6.6 %collective-permute-start = (bf16[1536,1024]{1,0:T(8,128)(2,1)}, bf16[1536,1024]{1,0:T(8,128)(2,1)}, u32[]{:S(2)}, u32[]{:S(2)}) collective-permute-start(bf16[1536,1024]{1,0:T(8,128)(2,1)} %fusion.9.blk_ref), channel_id=1, source_target_pairs={{0,4},{4,8},{8,12},{1,5},{5,9},{9,13},{2,6},{6,10},{10,14},{3,7},{... | collective-permute-start | bytes 9437192 | tf_op jit(solution)/shard_map/ppermute | solution.py:177
  24.8 1.3 collective-permute-start.2
  26.2 4.6 fusion.1
  31.5 75.5 %all-gather = f32[128,768]{1,0:T(8,128)S(1)} all-gather(f32[32,768]{1,0:T(8,128)S(1)} %pad_maximum_fusion), channel_id=2, replica_groups=mesh['part'=2,'loc'=4,'grp'=4] {'loc'}, dimensions={0}, use_global_device_ids=true | all-gather | bytes 491520 | tf_op jit(solution)/shard_map/all_gather | solution.py:166
  107.3 1.7 copy.59
  109.0 1.7 copy.60
  110.6 1.7 copy.62
  112.3 1.6 copy.61
  114.0 1.7 copy.64
  115.6 1.7 copy.63
  117.3 1.7 copy.65
  119.0 2.3 collective-permute-start.1
  121.3 1.7 collective-permute-start.4
  123.1 40.2 %shard_map.110 = (bf16[4,768,512]{2,1,0:T(8,128)(2,1)}, f32[4,768,1]{2,1,0:T(8,128)}, f32[4,3,512,896]{3,2,1,0:T(8,128)}) custom-call(s32[1]{0:T(128)} %bitcast.3.valid_ref, bf16[1536,1024]{1,0:T(8,128)(2,1)} %fusion.9.blk_ref, f32[4,768,2]{2,1,0:T(8,128)} %bitcast.86, bf16[4,512,896]{2,1,0:T(8,128)(2,1)} %all-gather.6.cloned.1.call-done.wg_ref, ...), custom_call_target="tpu_custom_call" | custom-call | flops 25367150592 | bytes 70000000 | tf_op jit(solution)/shard_map/pallas_call | solution.py:93
  163.3 8.2 %shard_map.111 = (bf16[4,768,512]{2,1,0:T(8,128)(2,1)}, f32[4,768,1]{2,1,0:T(8,128)}, f32[4,3,512,896]{3,2,1,0:T(8,128)}) custom-call(s32[1]{0:T(128)} %bitcast.8.valid_ref, bf16[1536,1024]{1,0:T(8,128)(2,1)} %collective-permute-done.blk_ref, f32[4,768,2]{2,1,0:T(8,128)} %bitcast.85, ...), custom_call_target="tpu_custom_call", output_to_operand_aliasing={{2}: (6, {})} | custom-call | flops 25367150592 | bytes 70000000 | tf_op jit(solution)/shard_map/pallas_call | solution.py:93
  171.5 42.6 %shard_map.112 = (bf16[4,768,512]{2,1,0:T(8,128)(2,1)}, f32[4,768,1]{2,1,0:T(8,128)}, f32[4,3,512,896]{3,2,1,0:T(8,128)}) custom-call(s32[1]{0:T(128)} %bitcast.16.valid_ref, bf16[1536,1024]{1,0:T(8,128)(2,1)} %collective-permute-done.2.blk_ref, f32[4,768,2]{2,1,0:T(8,128)} %bitcast.84, ...), custom_call_target="tpu_custom_call", output_to_operand_aliasing={{2}: (6, {})} | custom-call | flops 25367150592 | bytes 70000000 | tf_op jit(solution)/shard_map/pallas_call | solution.py:93
  214.1 2.3 collective-permute-start.3
  216.4 1.3 collective-permute-start.8
  217.7 8.2 %shard_map.113 = (bf16[4,768,512]{2,1,0:T(8,128)(2,1)}, f32[4,768,1]{2,1,0:T(8,128)}, f32[4,3,512,896]{3,2,1,0:T(8,128)}) custom-call(s32[1]{0:T(128)} %bitcast.12.valid_ref, bf16[1536,1024]{1,0:T(8,128)(2,1)} %collective-permute-done.1.blk_ref, f32[4,768,2]{2,1,0:T(8,128)} %bitcast.83, ...), custom_call_target="tpu_custom_call", output_to_operand_aliasing={{2}: (6, {})} | custom-call | flops 25367150592 | bytes 70000000 | tf_op jit(solution)/shard_map/pallas_call | solution.py:93
  225.9 42.9 %shard_map.114 = (bf16[4,768,512]{2,1,0:T(8,128)(2,1)}, f32[4,768,1]{2,1,0:T(8,128)}, f32[4,3,512,896]{3,2,1,0:T(8,128)}) custom-call(s32[1]{0:T(128)} %bitcast.24.valid_ref, bf16[1536,1024]{1,0:T(8,128)(2,1)} %copy-done.17, f32[4,768,2]{2,1,0:T(8,128)} %bitcast.82, ...), custom_call_target="tpu_custom_call", output_to_operand_aliasing={{2}: (6, {})} | custom-call | flops 25367150592 | bytes 70000000 | tf_op jit(solution)/shard_map/pallas_call | solution.py:93
  268.8 8.2 %shard_map.115 = (bf16[4,768,512]{2,1,0:T(8,128)(2,1)}, f32[4,768,1]{2,1,0:T(8,128)}, f32[4,3,512,896]{3,2,1,0:T(8,128)}) custom-call(s32[1]{0:T(128)} %bitcast.20.valid_ref, bf16[1536,1024]{1,0:T(8,128)(2,1)} %collective-permute-done.3.blk_ref, f32[4,768,2]{2,1,0:T(8,128)} %bitcast.81, ...), custom_call_target="tpu_custom_call", output_to_operand_aliasing={{2}: (6, {})} | custom-call | flops 25367150592 | bytes 70000000 | tf_op jit(solution)/shard_map/pallas_call | solution.py:93
  276.9 42.1 %collective-permute-done.8.blk_ref = bf16[1536,1024]{1,0:T(8,128)(2,1)} collective-permute-done((bf16[1536,1024]{1,0:T(8,128)(2,1)S(1)}, bf16[1536,1024]{1,0:T(8,128)(2,1)}, u32[]{:S(2)}, u32[]{:S(2)}) %collective-permute-start.8) | collective-permute-done | bytes 3145760 | tf_op jit(solution)/shard_map/ppermute | solution.py:178
  319.0 42.5 %shard_map.116 = (bf16[4,768,512]{2,1,0:T(8,128)(2,1)}, f32[4,768,1]{2,1,0:T(8,128)}, f32[4,3,512,896]{3,2,1,0:T(8,128)}) custom-call(s32[1]{0:T(128)} %bitcast.28.valid_ref, bf16[1536,1024]{1,0:T(8,128)(2,1)} %collective-permute-done.8.blk_ref, f32[4,768,2]{2,1,0:T(8,128)} %bitcast.80, ...), custom_call_target="tpu_custom_call", output_to_operand_aliasing={{2}: (6, {})} | custom-call | flops 25367150592 | bytes 70000000 | tf_op jit(solution)/shard_map/pallas_call | solution.py:93
  361.6 1.0 collective-permute-start.5
  362.6 1.5 collective-permute-start.9
  364.1 0.9 add_convert_fusion.3
  365.0 0.9 collective-permute-start.6
  365.9 60.9 %collective-permute-done.9 = bf16[4,768,512]{2,1,0:T(8,128)(2,1)S(1)} collective-permute-done((bf16[4,768,512]{2,1,0:T(8,128)(2,1)}, bf16[4,768,512]{2,1,0:T(8,128)(2,1)S(1)}, u32[]{:S(2)}, u32[]{:S(2)}) %collective-permute-start.9) | collective-permute-done | bytes 3145760 | tf_op jit(solution)/shard_map/ppermute | solution.py:201
  426.8 1.0 add_convert_fusion.1
  427.8 4.9 collective-permute-start.10
  432.7 2.6 add_convert_fusion.2
  435.3 1.3 collective-permute-start.7
  436.5 57.8 %collective-permute-done.10 = bf16[4,768,512]{2,1,0:T(8,128)(2,1)S(1)} collective-permute-done((bf16[4,768,512]{2,1,0:T(8,128)(2,1)S(1)}, bf16[4,768,512]{2,1,0:T(8,128)(2,1)S(1)}, u32[]{:S(2)}, u32[]{:S(2)}) %collective-permute-start.10) | collective-permute-done | bytes 3145760 | tf_op jit(solution)/shard_map/ppermute | solution.py:201
  494.4 2.6 add_convert_fusion
  497.0 15.4 %collective-permute-start.11 = (bf16[4,768,512]{2,1,0:T(8,128)(2,1)}, bf16[4,768,512]{2,1,0:T(8,128)(2,1)}, u32[]{:S(2)}, u32[]{:S(2)}) collective-permute-start(bf16[4,768,512]{2,1,0:T(8,128)(2,1)} %add_convert_fusion), channel_id=1, source_target_pairs={{0,4},{4,8},{8,12},{1,5},{5,9},{9,13},{2,6},{6,10},{10,14},{3,7},{... | collective-permute-start | bytes 9437192 | tf_op jit(solution)/shard_map/ppermute | solution.py:201
  513.4 2.0 reduce.4
  516.5 1.9 reduce.3
  518.9 67.1 %all-gather.1 = f32[28,4,768,1]{2,1,3,0:T(4,128)S(1)} all-gather(f32[7,4,768,1]{2,1,3,0:T(4,128)S(1)} %constant_dynamic-update-slice_fusion), channel_id=3, replica_groups=mesh['part'=2,'loc'=4,'grp'=4] {'loc'}, dimensions={0}, use_global_device_ids=true | all-gather | bytes 430080 | tf_op jit(solution)/shard_map/all_gather | solution.py:219
  586.4 4.3 fusion.2
  590.7 0.7 select_reduce_fusion.2
  591.4 4.4 select_reduce_fusion.1
  595.8 3.9 fusion.13
  599.7 2.8 convert_element_type.105
  602.5 1.4 slice_bitcast_fusion
  604.0 1.3 copy.58
  (104 shorter events, 6.6 us)
Async XLA Ops:
  7.2 115.9 %all-gather.10.cloned.1.call-start = ((), (), s32[]{:S(2)}) async-start(), calls=%async_computation.3 | async-start | bytes 4587520 | tf_op jit(solution)/shard_map/all_gather | solution.py:172
  7.9 3.8 copy-start.18
  7.9 3.8 copy-start.19
  7.9 115.1 %all-gather.6.cloned.1.call-start = ((), (), s32[]{:S(2)}) async-start(), calls=%async_computation.1 | async-start | bytes 4587520 | tf_op jit(solution)/shard_map/all_gather | solution.py:170
  8.7 114.4 %all-gather.8.cloned.1.call-start = ((), (), s32[]{:S(2)}) async-start(), calls=%async_computation.2 | async-start | bytes 4587520 | tf_op jit(solution)/shard_map/all_gather | solution.py:171
  9.4 590.3 %reduce-scatter.2.cloned.1.call-start = ((), (), s32[]{:S(2)}) async-start(), calls=%async_computation.4 | async-start | bytes 27525120 | tf_op jit(solution)/shard_map/reduce_scatter | solution.py:203
  11.7 14.5 %copy-start.15 = (s32[1536]{0:T(1024)}, s32[1536]{0:T(1024)S(1)}, u32[]{:S(2)}) copy-start(s32[1536]{0:T(1024)S(1)} %convert_element_type.86) | copy-start | bytes 18436
  11.8 14.3 %copy-start.12 = (s32[1536,4]{0,1:T(4,128)S(1)}, s32[1536,4]{0,1:T(4,128)}, u32[]{:S(2)}) copy-start(s32[1536,4]{0,1:T(4,128)} %param.9) | copy-start | bytes 73732
  11.8 14.4 %copy-start.14 = (f32[1536,4]{0,1:T(4,128)S(1)}, f32[1536,4]{0,1:T(4,128)}, u32[]{:S(2)}) copy-start(f32[1536,4]{0,1:T(4,128)} %param.10) | copy-start | bytes 73732
  18.2 100.8 %collective-permute-start = (bf16[1536,1024]{1,0:T(8,128)(2,1)}, bf16[1536,1024]{1,0:T(8,128)(2,1)}, u32[]{:S(2)}, u32[]{:S(2)}) collective-permute-start(bf16[1536,1024]{1,0:T(8,128)(2,1)} %fusion.9.blk_ref), channel_id=1, source_target_pairs={{0,4},{4,8},{8,12},{1,5},{5,9},{9,13},{2,6},{6,10},{10,14},{3,7},{... | collective-permute-start | bytes 9437192 | tf_op jit(solution)/shard_map/ppermute | solution.py:177
  24.8 96.5 %collective-permute-start.2 = (bf16[1536,1024]{1,0:T(8,128)(2,1)}, bf16[1536,1024]{1,0:T(8,128)(2,1)}, u32[]{:S(2)}, u32[]{:S(2)}) collective-permute-start(bf16[1536,1024]{1,0:T(8,128)(2,1)} %fusion.9.blk_ref), channel_id=1, source_target_pairs={{4,0},{8,4},{12,8},{5,1},{9,5},{13,9},{6,2},{10,6},{14,10},{7,3},{... | collective-permute-start | bytes 9437192 | tf_op jit(solution)/shard_map/ppermute | solution.py:178
  30.9 0.6 copy-start.10
  119.0 95.1 %collective-permute-start.1 = (bf16[1536,1024]{1,0:T(8,128)(2,1)}, bf16[1536,1024]{1,0:T(8,128)(2,1)}, u32[]{:S(2)}, u32[]{:S(2)}) collective-permute-start(bf16[1536,1024]{1,0:T(8,128)(2,1)} %collective-permute-done.blk_ref), channel_id=1, source_target_pairs={{4,8},{8,12},{5,9},{9,13},{6,10},{10,14},{7,11},{11,15},{20,24},{2... | collective-permute-start | bytes 9437192 | tf_op jit(solution)/shard_map/ppermute | solution.py:177
  121.3 95.1 %collective-permute-start.4 = (bf16[1536,1024]{1,0:T(8,128)(2,1)}, bf16[1536,1024]{1,0:T(8,128)(2,1)S(1)}, u32[]{:S(2)}, u32[]{:S(2)}) collective-permute-start(bf16[1536,1024]{1,0:T(8,128)(2,1)} %collective-permute-done.2.blk_ref), channel_id=1, source_target_pairs={{4,0},{8,4},{5,1},{9,5},{6,2},{10,6},{7,3},{11,7},{20,16},{24,20},... | collective-permute-start | bytes 9437192 | tf_op jit(solution)/shard_map/ppermute | solution.py:178
  214.1 54.7 %collective-permute-start.3 = (bf16[1536,1024]{1,0:T(8,128)(2,1)}, bf16[1536,1024]{1,0:T(8,128)(2,1)}, u32[]{:S(2)}, u32[]{:S(2)}) collective-permute-start(bf16[1536,1024]{1,0:T(8,128)(2,1)} %collective-permute-done.1.blk_ref), channel_id=1, source_target_pairs={{8,12},{9,13},{10,14},{11,15},{24,28},{25,29},{26,30},{27,31}} | collective-permute-start | bytes 9437192 | tf_op jit(solution)/shard_map/ppermute | solution.py:177
  216.4 9.5 %copy-start.17 = (bf16[1536,1024]{1,0:T(8,128)(2,1)}, bf16[1536,1024]{1,0:T(8,128)(2,1)S(1)}, u32[]{:S(2)}) copy-start(bf16[1536,1024]{1,0:T(8,128)(2,1)S(1)} %collective-permute-done.4.blk_ref) | copy-start | bytes 9437188
  216.4 102.6 %collective-permute-start.8 = (bf16[1536,1024]{1,0:T(8,128)(2,1)S(1)}, bf16[1536,1024]{1,0:T(8,128)(2,1)}, u32[]{:S(2)}, u32[]{:S(2)}) collective-permute-start(bf16[1536,1024]{1,0:T(8,128)(2,1)S(1)} %collective-permute-done.4.blk_ref), channel_id=1, source_target_pairs={{4,0},{5,1},{6,2},{7,3},{20,16},{21,17},{22,18},{23,19}} | collective-permute-start | bytes 9437192 | tf_op jit(solution)/shard_map/ppermute | solution.py:178
  361.5 2.5 copy-start.4
  361.6 2.5 collective-permute-start.5
  362.6 64.2 %collective-permute-start.9 = (bf16[4,768,512]{2,1,0:T(8,128)(2,1)}, bf16[4,768,512]{2,1,0:T(8,128)(2,1)S(1)}, u32[]{:S(2)}, u32[]{:S(2)}) collective-permute-start(bf16[4,768,512]{2,1,0:T(8,128)(2,1)} %get-tuple-element.38), channel_id=1, source_target_pairs={{0,4},{1,5},{2,6},{3,7},{16,20},{17,21},{18,22},{19,23}} | collective-permute-start | bytes 9437192 | tf_op jit(solution)/shard_map/ppermute | solution.py:201
  364.1 62.7 %copy-start.3 = (bf16[4,768,512]{2,1,0:T(8,128)(2,1)S(1)}, bf16[4,768,512]{2,1,0:T(8,128)(2,1)}, u32[]{:S(2)}) copy-start(bf16[4,768,512]{2,1,0:T(8,128)(2,1)} %get-tuple-element.36) | copy-start | bytes 9437188
  365.0 67.6 %collective-permute-start.6 = (bf16[4,768,512]{2,1,0:T(8,128)(2,1)S(1)}, bf16[4,768,512]{2,1,0:T(8,128)(2,1)S(1)}, u32[]{:S(2)}, u32[]{:S(2)}) collective-permute-start(bf16[4,768,512]{2,1,0:T(8,128)(2,1)S(1)} %add_convert_fusion.3), channel_id=1, source_target_pairs={{8,4},{12,8},{9,5},{13,9},{10,6},{14,10},{11,7},{15,11},{24,20},{2... | collective-permute-start | bytes 9437192 | tf_op jit(solution)/shard_map/ppermute | solution.py:199
  426.8 5.9 copy-start.2
  427.8 66.6 %collective-permute-start.10 = (bf16[4,768,512]{2,1,0:T(8,128)(2,1)S(1)}, bf16[4,768,512]{2,1,0:T(8,128)(2,1)S(1)}, u32[]{:S(2)}, u32[]{:S(2)}) collective-permute-start(bf16[4,768,512]{2,1,0:T(8,128)(2,1)S(1)} %add_convert_fusion.1), channel_id=1, source_target_pairs={{0,4},{4,8},{1,5},{5,9},{2,6},{6,10},{3,7},{7,11},{16,20},{20,24},... | collective-permute-start | bytes 9437192 | tf_op jit(solution)/shard_map/ppermute | solution.py:201
  432.7 61.7 %copy-start.1 = (bf16[4,768,512]{2,1,0:T(8,128)(2,1)S(1)}, bf16[4,768,512]{2,1,0:T(8,128)(2,1)}, u32[]{:S(2)}) copy-start(bf16[4,768,512]{2,1,0:T(8,128)(2,1)} %get-tuple-element.35) | copy-start | bytes 9437188
  435.3 156.1 %collective-permute-start.7 = (bf16[4,768,512]{2,1,0:T(8,128)(2,1)}, bf16[4,768,512]{2,1,0:T(8,128)(2,1)}, u32[]{:S(2)}, u32[]{:S(2)}) collective-permute-start(bf16[4,768,512]{2,1,0:T(8,128)(2,1)} %add_convert_fusion.2), channel_id=1, source_target_pairs={{4,0},{8,4},{12,8},{5,1},{9,5},{13,9},{6,2},{10,6},{14,10},{7,3},{... | collective-permute-start | bytes 9437192 | tf_op jit(solution)/shard_map/ppermute | solution.py:199
  494.3 18.1 %copy-start.6 = (f32[4,768,1]{2,1,0:T(8,128)S(1)}, f32[4,768,1]{2,1,0:T(8,128)}, u32[]{:S(2)}) copy-start(f32[4,768,1]{2,1,0:T(8,128)} %get-tuple-element.40) | copy-start | bytes 36868
  494.4 18.6 %copy-start.5 = (f32[4,768,1]{2,1,0:T(8,128)S(1)}, f32[4,768,1]{2,1,0:T(8,128)}, u32[]{:S(2)}) copy-start(f32[4,768,1]{2,1,0:T(8,128)} %get-tuple-element.39) | copy-start | bytes 36868
  497.0 94.4 %collective-permute-start.11 = (bf16[4,768,512]{2,1,0:T(8,128)(2,1)}, bf16[4,768,512]{2,1,0:T(8,128)(2,1)}, u32[]{:S(2)}, u32[]{:S(2)}) collective-permute-start(bf16[4,768,512]{2,1,0:T(8,128)(2,1)} %add_convert_fusion), channel_id=1, source_target_pairs={{0,4},{4,8},{8,12},{1,5},{5,9},{9,13},{2,6},{6,10},{10,14},{3,7},{... | collective-permute-start | bytes 9437192 | tf_op jit(solution)/shard_map/ppermute | solution.py:201
  512.9 2.6 copy-start.7
  513.4 2.6 copy-start.8
  515.9 2.4 copy-start.9
  516.0 70.3 %copy-start.11 = (f32[16,768]{1,0:T(8,128)S(1)}, f32[16,768]{1,0:T(8,128)}, u32[]{:S(2)}) copy-start(f32[16,768]{1,0:T(8,128)} %copy-done.10) | copy-start | bytes 147460
  516.0 70.4 %copy-start.16 = (s32[1536]{0:T(1024)S(1)}, s32[1536]{0:T(1024)}, u32[]{:S(2)}) copy-start(s32[1536]{0:T(1024)} %copy-done.15) | copy-start | bytes 18436
  518.9 71.8 %copy-start.13 = (s32[1536,4]{0,1:T(4,128)S(1)}, s32[1536,4]{0,1:T(4,128)}, u32[]{:S(2)}) copy-start(s32[1536,4]{0,1:T(4,128)} %param.9) | copy-start | bytes 73732
  518.9 72.5 %copy-start = (bf16[4,768,512]{2,1,0:T(8,128)(2,1)S(1)}, bf16[4,768,512]{2,1,0:T(8,128)(2,1)}, u32[]{:S(2)}) copy-start(bf16[4,768,512]{2,1,0:T(8,128)(2,1)} %get-tuple-element.26) | copy-start | bytes 9437188
Sparse Core Ops, SparseCore 0:
  9.5 34.0 all-gather.9
  45.1 31.2 all-gather.5
  78.0 31.2 all-gather.7
  361.7 162.2 reduce-scatter.1
